TPU v7x, 128 devices: a whole 4x4x4 slice. The times are simulated.
128 devices in a mesh: mem: 16 (over y, x), pix: 8 (over z, core).
Axes of the slice: x: 4, y: 4, z: 4, core: 2. Of those that a mesh axis runs over, the one named last changes fastest.
Arguments:
- prior_motion: bfloat16 [64, 16, 262144], P('mem', None, 'pix'), may hold values from -6 to 6
- measured_motion: float32 [1200], replicated, may hold values from -1.6 to 1.6
- measurement_noise_stddev: float32 [1200], replicated, may hold values from 0.05 to 0.5
- gaussian_jitter: float32 [2, 1200, 64], replicated, may hold values from -6 to 6
- scene_couples: int32 [2, 1200], replicated, may hold values from 0 to 15, as said below
- targeted_tile_number: int32 [1200], replicated, may hold values from 0 to 4095
Outputs:
- analysis: bfloat16 [64, 16, 262144], P('mem', None, 'pix')
Inputs may be any that keep to these rules, and one draw needn't show every extreme that they name: scene_couples[0, k] < scene_couples[1, k]: row 0 holds the earlier acquisition, row 1 the later.
All inputs are finite; a program needn't handle non-finite values.
Results may differ from a plain program's by a relative error of at most 0.011.
Values may be sent and summed in bfloat16 or wider, within the bound.
No kernel may reach another device: no remote copies, remote signals or barrier semaphores. Data moves between devices by JAX's collectives and lax.ppermute only.
A program may use at most 128 MiB of HBM per device.

v0:
```python
import math

import jax
import jax.numpy as jnp
from jax import lax
from jax.sharding import PartitionSpec as P

BLK = 64
PASS_COUNT = 2


def block_sums(pieces):
    part_cells = pieces.shape[2]
    block_count = part_cells // BLK
    summer = (
        jnp.arange(part_cells, dtype=jnp.int32)[:, None] // BLK
        == jnp.arange(block_count, dtype=jnp.int32)[None, :]
    ).astype(jnp.bfloat16)
    flat = jnp.dot(pieces.reshape(-1, part_cells), summer, preferred_element_type=jnp.float32)
    return flat.reshape(pieces.shape[0], pieces.shape[1], block_count)


def with_sums(pieces):
    return (pieces, block_sums(pieces))


def to_pixels(ground_motion_vector):
    return with_sums(
        lax.all_to_all(ground_motion_vector, "mem", split_axis=2, concat_axis=0, tiled=True)
    )


def to_members(pixel_state):
    return lax.all_to_all(pixel_state, "mem", split_axis=0, concat_axis=2, tiled=True)


def predict(sums, picker):
    flat_sums = sums.reshape(sums.shape[0], -1)
    return (
        jnp.dot(
            picker, flat_sums.T, precision=lax.Precision.HIGHEST, preferred_element_type=jnp.float32
        )
        / BLK
    )


def member_terms(predicted, measured_motion, member_anomaly, noise):
    realization_vectors = predicted.shape[1]
    centred = predicted - jnp.mean(predicted, axis=1, keepdims=True)
    scaled = centred / (member_anomaly[:, None] * math.sqrt(realization_vectors - 1))
    misfit = (
        measured_motion[:, None] + member_anomaly[:, None] * noise - predicted
    ) / member_anomaly[:, None]
    return (scaled, misfit)


def products(scaled, misfit):
    gram = jnp.dot(
        scaled.T, scaled, precision=lax.Precision.HIGHEST, preferred_element_type=jnp.float32
    )
    cross = jnp.dot(
        scaled.T, misfit, precision=lax.Precision.HIGHEST, preferred_element_type=jnp.float32
    )
    return (gram, cross)


def solve_mixing(gram, cross):
    realization_vectors = gram.shape[0]
    factor = jnp.linalg.cholesky(jnp.eye(realization_vectors, dtype=jnp.float32) + gram)
    return (
        jax.scipy.linalg.cho_solve((factor, True), cross) / math.sqrt(realization_vectors - 1)
    ).astype(jnp.bfloat16)


def update(pixel_state, mixing):
    realization_vectors = pixel_state.shape[0]
    average = jnp.sum(pixel_state, axis=0, dtype=jnp.float32) / realization_vectors
    anomaly = (pixel_state.astype(jnp.float32) - average).astype(jnp.bfloat16)
    change = jnp.dot(
        mixing.T, anomaly.reshape(realization_vectors, -1), preferred_element_type=jnp.float32
    )
    return (pixel_state.astype(jnp.float32) + change.reshape(pixel_state.shape)).astype(
        jnp.bfloat16
    )


def body(
    prior_motion,
    measured_motion,
    measurement_noise_stddev,
    gaussian_jitter,
    scene_couples,
    targeted_tile_number,
):
    cells_per_tile = prior_motion.shape[2]
    part_width = cells_per_tile // lax.axis_size("mem")
    local_blocks = part_width // BLK
    first_block = (
        lax.axis_index("pix") * cells_per_tile + lax.axis_index("mem") * part_width
    ) // BLK
    block_range = first_block + jnp.arange(local_blocks, dtype=jnp.int32)
    block_table = (targeted_tile_number[:, None] == block_range[None, :]).astype(jnp.float32)
    scene_timeline = jnp.arange(prior_motion.shape[1], dtype=jnp.int32)
    pair_table = (scene_timeline[None, :] == scene_couples[1][:, None]).astype(jnp.float32) - (
        scene_timeline[None, :] == scene_couples[0][:, None]
    ).astype(jnp.float32)
    picker = (pair_table[:, :, None] * block_table[:, None, :]).reshape(pair_table.shape[0], -1)
    member_anomaly = jnp.sqrt(jnp.float32(float(PASS_COUNT))) * measurement_noise_stddev
    pixel_state, sums = to_pixels(prior_motion)
    for iteration in range(PASS_COUNT):
        if iteration > 0:
            sums = block_sums(pixel_state)
        predicted = predict(sums, picker)
        scaled, misfit = member_terms(
            predicted, measured_motion, member_anomaly, gaussian_jitter[iteration]
        )
        gram, cross = lax.psum(products(scaled, misfit), ("mem", "pix"))
        pixel_state = update(pixel_state, solve_mixing(gram, cross))
    return to_members(pixel_state)


def solution(mesh):
    return jax.shard_map(
        body,
        mesh=mesh,
        in_specs=(P("mem", None, "pix"), P(), P(), P(), P(), P()),
        out_specs=P("mem", None, "pix"),
        check_vma=False,
    )
```

profile of v0, /device:TPU:0, one launch (start us, length us, event | category | flops | bytes accessed | tf_op | source)
XLA Modules:
  0.0 537.4 jit_solution(16468579744521945431)
XLA Ops:
  0.0 37.7 %copy.41 = bf16[4,16,32768]{1,0,2:T(4,128)(2,1)} copy(bf16[4,16,32768]{2,1,0:T(8,128)(2,1)} %param.9) | data formatting | bytes 8388608 | tf_op args[0]
  37.7 36.8 %reshape.195 = bf16[16,2,65536]{2,1,0:T(2,128)(2,1)} reshape(bf16[32768,4,16]{2,1,0:T(4,128)(2,1)} %bitcast.107) | data formatting | bytes 8388608
  74.6 0.0 copy-start.4
  74.6 7.3 %all-to-all-start = ((bf16[16,2,65536]{2,1,0:T(2,128)(2,1)}), bf16[16,2,65536]{2,1,0:T(2,128)(2,1)}, u32[]{:S(2)}, u32[]{:S(2)}) async-start(bf16[16,2,65536]{2,1,0:T(2,128)(2,1)} %reshape.195), calls=%async_computation | async-start | bytes 8388608 | tf_op jit(solution)/shard_map/all_to_all | solution.py:29
  82.0 0.0 copy-done.4
  82.0 0.0 copy-done.6
  82.1 0.1 compare_convert_fusion
  82.1 0.2 broadcast_multiply_fusion
  82.4 62.8 %all-to-all-done = bf16[16,2,65536]{2,1,0:T(2,128)(2,1)} async-done(((bf16[16,2,65536]{2,1,0:T(2,128)(2,1)}), bf16[16,2,65536]{2,1,0:T(2,128)(2,1)}, u32[]{:S(2)}, u32[]{:S(2)}) %all-to-all-start) | async-done | bytes 4194336 | tf_op jit(solution)/shard_map/all_to_all | solution.py:29
  145.2 25.6 %reshape.196 = bf16[32768,4,16]{2,1,0:T(4,128)(2,1)} reshape(bf16[16,2,65536]{2,1,0:T(2,128)(2,1)} %all-to-all-done) | data formatting | bytes 8388608
  170.8 44.3 %copy.66 = bf16[4,16,16,2048]{3,1,0,2:T(8,128)(2,1)} copy(bf16[4,16,16,2048]{1,0,3,2:T(4,128)(2,1)} %bitcast.105) | data formatting | bytes 8388608 | tf_op jit(solution)/shard_map/all_to_all | solution.py:29
  215.1 33.4 %copy.65 = bf16[4,16,16,2048]{3,2,1,0:T(8,128)(2,1)} copy(bf16[4,16,16,2048]{1,0,3,2:T(4,128)(2,1)} %bitcast.106) | data formatting | bytes 8388608 | tf_op jit(solution)/shard_map/all_to_all | solution.py:29
  248.5 0.0 copy-start.1
  248.5 3.4 bitcast_convert_fusion
  251.9 0.0 copy-done.1
  252.0 0.9 fusion.7
  252.9 2.3 copy-done
  255.2 8.1 %copy.48 = f32[16,4,16,2048]{3,2,1,0:T(8,128)} copy(f32[16,4,16,2048]{3,0,2,1:T(8,128)S(1)} %bitcast_convert_fusion) | data formatting | bytes 16777216 | tf_op jit(solution)/shard_map/convert_element_type | solution.py:82
  263.3 12.4 %copy.43 = f32[16,4,16,2048]{3,1,0,2:T(4,128)} copy(f32[16,4,16,2048]{3,0,2,1:T(8,128)} %copy-done) | data formatting | bytes 16777216 | tf_op jit(solution)/shard_map/convert_element_type | solution.py:82
  275.7 3.5 convolution_bitcast_fusion
  279.2 0.2 copy.45
  279.5 0.2 reshape_reshape.6
  279.7 0.0 copy-start.7
  279.7 1.8 fusion.56
  281.5 0.0 copy-done.5
  281.5 0.4 fusion.29
  281.9 0.0 copy-done.9
  282.0 0.0 copy-done.7
  282.0 0.5 fusion.25
  282.4 65.0 %all-reduce.1 = (f32[64,64]{1,0:T(8,128)S(1)}, f32[64,64]{0,1:T(8,128)S(1)}) all-reduce(f32[64,64]{1,0:T(8,128)S(1)} %fusion.25, f32[64,64]{0,1:T(8,128)S(1)} %fusion.29), channel_id=1, replica_groups=mesh['mem'=16,'pix'=8] {'mem','pix'}, use_global_device_ids=true, to_apply=%region_4.6 | all-reduce | flops 8192 | bytes 65536 | tf_op jit(solution)/shard_map/psum | solution.py:117
  347.5 0.1 copy.47
  347.6 5.8 %cholesky.44 = f32[64,64]{1,0:T(8,128)S(1)} custom-call(f32[64,64]{1,0:T(8,128)S(1)} %fusion.52), custom_call_target="Cholesky" | custom-call | tf_op jit(solution)/shard_map/jit(cholesky)/cholesky | solution.py:69
  353.5 0.6 compare_reduce_fusion.1
  354.1 0.7 fusion.43
  354.8 4.9 custom-call.8
  359.7 0.3 fusion.50
  359.9 0.2 fusion.11
  360.1 11.6 %copy.73 = f32[8,8,16,2048]{3,1,2,0:T(8,128)} copy(f32[8,8,16,2048]{3,2,1,0:T(8,128)} %bitcast.108) | data formatting | bytes 16777216
  371.8 10.4 %reshape.189 = f32[64,16,2048]{2,0,1:T(8,128)} reshape(f32[16,4,16,2048]{3,1,0,2:T(4,128)} %copy.43) | data formatting | bytes 16777216 | tf_op jit(solution)/shard_map/convert_element_type | solution.py:82
  382.2 0.0 copy-start.2
  382.2 4.1 subtract_convert_fusion
  386.3 1.7 copy-done.2
  388.0 1.4 convert_reduce_fusion
  389.3 0.0 copy-start.3
  389.4 2.3 copy.51
  391.7 0.0 copy-done.3
  391.7 1.4 fusion.12
  393.0 0.2 reshape_reshape.7
  393.3 1.8 fusion.57
  395.1 0.4 fusion.30
  395.5 0.0 copy-done.8
  395.5 0.5 fusion.20
  396.0 64.3 %all-reduce = (f32[64,64]{1,0:T(8,128)S(1)}, f32[64,64]{0,1:T(8,128)S(1)}) all-reduce(f32[64,64]{1,0:T(8,128)S(1)} %fusion.20, f32[64,64]{0,1:T(8,128)S(1)} %fusion.30), channel_id=1, replica_groups=mesh['mem'=16,'pix'=8] {'mem','pix'}, use_global_device_ids=true, to_apply=%region_8.11 | all-reduce | flops 8192 | bytes 65536 | tf_op jit(solution)/shard_map/psum | solution.py:117
  460.4 0.1 copy.54
  460.5 5.8 %cholesky.55 = f32[64,64]{1,0:T(8,128)S(1)} custom-call(f32[64,64]{1,0:T(8,128)S(1)} %fusion.48), custom_call_target="Cholesky" | custom-call | tf_op jit(solution)/shard_map/jit(cholesky)/cholesky | solution.py:69
  466.3 0.7 compare_reduce_fusion
  467.1 0.7 fusion.44
  467.8 4.9 custom-call.9
  472.7 0.3 fusion.46
  472.9 0.2 fusion.10
  473.1 5.0 fusion.1
  478.2 2.3 copy.58
  480.5 54.4 %all_to_all.33 = bf16[64,16,2048]{2,1,0:T(8,128)(2,1)S(1)} all-to-all(bf16[64,16,2048]{2,1,0:T(8,128)(2,1)S(1)} %copy.58), channel_id=1, replica_groups=mesh['mem'=16,'pix'=8] {'mem'}, dimensions={0} | all-to-all | bytes 8388608 | tf_op jit(solution)/shard_map/all_to_all | solution.py:34
  534.9 2.3 copy.72
  (20 shorter events, 0.2 us)
Async XLA Ops:
  74.6 7.4 %copy-start.4 = (s32[2,1200]{1,0:T(2,128)S(1)}, s32[2,1200]{1,0:T(2,128)}, u32[]{:S(2)}) copy-start(s32[2,1200]{1,0:T(2,128)} %param.13) | copy-start | bytes 28804
  74.6 7.5 %copy-start.6 = (s32[1200]{0:T(1024)S(1)}, s32[1200]{0:T(1024)}, u32[]{:S(2)}) copy-start(s32[1200]{0:T(1024)} %param.14) | copy-start | bytes 14404
  74.6 70.6 %all-to-all-start = ((bf16[16,2,65536]{2,1,0:T(2,128)(2,1)}), bf16[16,2,65536]{2,1,0:T(2,128)(2,1)}, u32[]{:S(2)}, u32[]{:S(2)}) async-start(bf16[16,2,65536]{2,1,0:T(2,128)(2,1)} %reshape.195), calls=%async_computation | async-start | bytes 8388608 | tf_op jit(solution)/shard_map/all_to_all | solution.py:29
  248.5 3.5 copy-start.1
  252.0 3.2 copy-start
  275.7 5.8 %copy-start.5 = (f32[1200]{0:T(1024)S(1)}, f32[1200]{0:T(1024)}, u32[]{:S(2)}) copy-start(f32[1200]{0:T(1024)} %param.11) | copy-start | bytes 14404
  275.7 6.3 %copy-start.9 = (f32[1200]{0:T(1024)S(1)}, f32[1200]{0:T(1024)}, u32[]{:S(2)}) copy-start(f32[1200]{0:T(1024)} %param.10) | copy-start | bytes 14404
  279.7 2.3 copy-start.7
  382.2 5.8 %copy-start.2 = (f32[64,16,2048]{2,0,1:T(8,128)S(1)}, f32[64,16,2048]{2,0,1:T(8,128)}, u32[]{:S(2)}) copy-start(f32[64,16,2048]{2,0,1:T(8,128)} %reshape.189) | copy-start | bytes 25165828
  389.3 2.3 copy-start.3
  393.3 2.2 copy-start.8
where the time goes:
time: 546 us; the launch traced here: 537 us
  local copies, waits for them, and re-layouts  232 us (42%)
  blocking collectives  184 us (34%)
  waiting for transfers between devices  62.8 us (12%)
  other arithmetic  33.1 us (6%)
  matrix products  17.5 us (3%)
  starting transfers between devices  7.33 us (1%)
    psum x2, blocking collectives, body(): gram, cross = lax.psum(products(scaled, misfit), ('mem', 'pix'))  129 us
    unnamed x25, local copies, waits for them, and re-layouts  116 us
    all_to_all x2, local copies, waits for them, and re-layouts, to_pixels(): lax.all_to_all(ground_motion_vector, 'mem', split_axis=2, concat_axis=0,...  77.7 us
    all_to_all x1, waiting for transfers between devices, to_pixels(): lax.all_to_all(ground_motion_vector, 'mem', split_axis=2, concat_axis=0,...  62.8 us
    all_to_all x1, blocking collectives, to_members(): lax.all_to_all(pixel_state, 'mem', split_axis=0, concat_axis=2, tiled=True)  54.4 us
    convert_element_type x3, local copies, waits for them, and re-layouts, update(): pixel_state.astype(jnp.float32) + change.reshape(pixel_state.shape)  30.9 us
    another operation x6, other arithmetic, solve_mixing(): jnp.linalg.cholesky(jnp.eye(realization_vectors, dtype=jnp.float32) + gram)  13.1 us
    another operation x4, other arithmetic, solve_mixing(): jax.scipy.linalg.cho_solve((factor, True), cross)  11.1 us
  transfers between devices with their start and end apart: 1, of which 1 were waited for; matrix products, arithmetic and copies ran while one was open for 0% of the time, Pallas kernels for 0%

commit v1 on v0

v1 whole, which is shorter than its diff:
```python
import math

import jax
import jax.numpy as jnp
from jax import lax
from jax.sharding import PartitionSpec as P

BLK = 64
PASS_COUNT = 2
HI = lax.Precision.HIGHEST


def mm(a, b):
    return jnp.dot(a, b, precision=HI, preferred_element_type=jnp.float32)


def tn(a, b):
    return lax.dot_general(
        a, b, (((0,), (0,)), ((), ())), precision=HI, preferred_element_type=jnp.float32
    )


def local_sums(parts):
    n_part, members, dates, width = parts.shape
    blocks = width // BLK
    summer = (
        jnp.arange(width, dtype=jnp.int32)[:, None] // BLK
        == jnp.arange(blocks, dtype=jnp.int32)[None, :]
    ).astype(jnp.bfloat16)
    flat = jnp.dot(parts.reshape(-1, width), summer, preferred_element_type=jnp.float32)
    flat = flat.reshape(n_part, members * dates, blocks)
    return jnp.moveaxis(flat, 0, 1).reshape(members * dates, n_part * blocks)


def local_predicted(sums, dates, first_block, scene_couples, targeted_tile_number):
    blocks = sums.shape[1]
    block_range = first_block + jnp.arange(blocks, dtype=jnp.int32)
    block_table = (block_range[:, None] == targeted_tile_number[None, :]).astype(jnp.float32)
    picked = mm(sums, block_table)
    timeline = jnp.arange(dates, dtype=jnp.int32)
    pair_table = (timeline[:, None] == scene_couples[1][None, :]).astype(jnp.float32) - (
        timeline[:, None] == scene_couples[0][None, :]
    ).astype(jnp.float32)
    picked = picked.reshape(-1, dates, picked.shape[1])
    return jnp.sum(picked * pair_table[None], axis=1) / BLK


def solve(gram, cross):
    n = gram.shape[0]
    factor = jnp.linalg.cholesky(jnp.eye(n, dtype=jnp.float32) + gram)
    mixing = jax.scipy.linalg.cho_solve((factor, True), cross) / math.sqrt(n - 1)
    return mixing.astype(jnp.bfloat16).astype(jnp.float32)


def combined_mixing(gram, cross_first, cross_second):
    n = gram.shape[0]
    first = solve(gram, cross_first)
    moved = first + jnp.eye(n, dtype=jnp.float32)
    moved = moved - jnp.mean(moved, axis=1, keepdims=True)
    gram_moved = mm(gram, moved)
    gram_next = tn(moved, gram_moved)
    cross_next = tn(moved, cross_second - math.sqrt(n - 1) * mm(gram, first))
    second = solve(gram_next, cross_next)
    whole = first + mm(moved, second)
    return whole - jnp.mean(whole, axis=0, keepdims=True)


def body(
    prior_motion,
    measured_motion,
    measurement_noise_stddev,
    gaussian_jitter,
    scene_couples,
    targeted_tile_number,
):
    members, dates, cells = prior_motion.shape
    n_mem = lax.axis_size("mem")
    width = cells // n_mem
    n = members * n_mem
    parts = jnp.moveaxis(prior_motion.reshape(members, dates, n_mem, width), 2, 0)
    state = lax.all_to_all(parts, "mem", split_axis=0, concat_axis=0, tiled=True)

    first_block = lax.axis_index("pix") * (cells // BLK)
    predicted = local_predicted(
        local_sums(parts), dates, first_block, scene_couples, targeted_tile_number
    )
    predicted = lax.all_gather(predicted, "mem", axis=0, tiled=True)
    in_tile = (targeted_tile_number // (cells // BLK)) == lax.axis_index("pix")
    spread = jnp.sqrt(jnp.float32(float(PASS_COUNT))) * measurement_noise_stddev
    scaled = (predicted - jnp.mean(predicted, axis=0, keepdims=True)) / (
        spread * math.sqrt(n - 1)
    )[None, :]
    fixed = (measured_motion[None, :] - predicted) / spread[None, :]
    misfits = [
        jnp.where(in_tile[None, :], fixed + gaussian_jitter[i].T, 0.0) for i in range(PASS_COUNT)
    ]
    right = jnp.concatenate([scaled] + misfits, axis=0)
    products = lax.dot_general(
        scaled, right, (((1,), (1,)), ((), ())), precision=HI, preferred_element_type=jnp.float32
    )
    products = lax.psum(products, "pix")
    mixing = combined_mixing(products[:, :n], products[:, n : 2 * n], products[:, 2 * n :])
    mixing = mixing.astype(jnp.bfloat16)

    rows = n * dates
    spread_mixing = (
        mixing.T[:, None, :, None] * jnp.eye(dates, dtype=jnp.bfloat16)[None, :, None, :]
    ).reshape(rows, rows)
    flat = state.reshape(rows, width)
    change = jnp.dot(spread_mixing, flat, preferred_element_type=jnp.float32)
    fresh = (flat.astype(jnp.float32) + change).astype(jnp.bfloat16)
    fresh = fresh.reshape(n_mem, members, dates, width)
    back = lax.all_to_all(fresh, "mem", split_axis=0, concat_axis=0, tiled=True)
    return jnp.moveaxis(back, 0, 2).reshape(members, dates, cells)


def solution(mesh):
    return jax.shard_map(
        body,
        mesh=mesh,
        in_specs=(P("mem", None, "pix"), P(), P(), P(), P(), P()),
        out_specs=P("mem", None, "pix"),
        check_vma=False,
    )
```

time: 546 us -> 243 us (0.45); the launches traced: 537 us -> 243 us
  local copies, waits for them, and re-layouts: 232 us -> 37.1 us
  waiting for transfers between devices: 62.8 us -> 0.01 us
  blocking collectives: 184 us -> 151 us
    unnamed x25 -> x11, local copies, waits for them, and re-layouts: 116 us -> 0.14 us
    psum x2 -> x1, blocking collectives: 129 us -> 25.5 us  [body(): products = lax.psum(products, 'pix')]
    all_to_all x3 -> x0, local copies, waits for them, and re-layouts: 80 us -> none  [the longest x2 77.7 us: to_pixels(): lax.all_to_all(ground_motion_vector, 'mem', split_axis=2, concat_axis=0,...]
    all_gather x0 -> x1, blocking collectives: none -> 72.2 us  [body(): predicted = lax.all_gather(predicted, 'mem', axis=0, tiled=True)]
    all_to_all x1, waiting for transfers between devices: 62.8 us -> 0.01 us  [body(): lax.all_to_all(parts, 'mem', split_axis=0, concat_axis=0, tiled=True)]
    convert_element_type x5 -> x0, local copies, waits for them, and re-layouts: 35.5 us -> none  [the longest x3 30.9 us: update(): pixel_state.astype(jnp.float32) + change.reshape(pixel_state.shape)]
    mul x0 -> x1, local copies, waits for them, and re-layouts: none -> 29.1 us  [body(): mixing.T[:, None, :, None]]
    reshape x0 -> x4, local copies, waits for them, and re-layouts: none -> 7.52 us  [the longest x1 4.79 us: body(): prior_motion.reshape(members, dates, n_mem, width)]
  transfers between devices with their start and end apart: 1 -> 1, of which waited for: 1 -> 0; matrix products, arithmetic and copies ran while one was open for 0% -> 28% of each run, Pallas kernels for 0% -> 0%
where the time goes in v1:
time: 243 us
  blocking collectives  151 us (62%)
  local copies, waits for them, and re-layouts  37.1 us (15%)
  other arithmetic  30.7 us (13%)
  matrix products  15.9 us (7%)
  starting transfers between devices  7.33 us (3%)
    all_gather x1, blocking collectives, body(): predicted = lax.all_gather(predicted, 'mem', axis=0, tiled=True)  72.2 us
    all_to_all x1, blocking collectives, body(): back = lax.all_to_all(fresh, 'mem', split_axis=0, concat_axis=0, tiled=True)  53.3 us
    mul x1, local copies, waits for them, and re-layouts, body(): mixing.T[:, None, :, None]  29.1 us
    psum x1, blocking collectives, body(): products = lax.psum(products, 'pix')  25.5 us
    another operation x6, other arithmetic, solve(): factor = jnp.linalg.cholesky(jnp.eye(n, dtype=jnp.float32) + gram)  13.2 us
    another operation x4, other arithmetic, solve(): jax.scipy.linalg.cho_solve((factor, True), cross) / math.sqrt(n - 1)  11.2 us
    dot_general x1, matrix products, body(): change = jnp.dot(spread_mixing, flat, preferred_element_type=jnp.float32)  8.04 us
    all_to_all x1, starting transfers between devices, body(): lax.all_to_all(parts, 'mem', split_axis=0, concat_axis=0, tiled=True)  7.33 us
  transfers between devices with their start and end apart: 1, of which 0 were waited for; matrix products, arithmetic and copies ran while one was open for 28% of the time, Pallas kernels for 0%

profile of v1, /device:TPU:0, one launch (start us, length us, event | category | flops | bytes accessed | tf_op | source)
XLA Modules:
  0.0 242.5 jit_solution(9956106009973401795)
XLA Ops:
  0.0 4.8 %copy.47 = bf16[4,2,16,8,2048]{4,3,1,0,2:T(8,128)(2,1)} copy(bf16[4,2,16,8,2048]{4,3,2,1,0:T(8,128)(2,1)} %bitcast.84) | data formatting | bytes 8388608 | tf_op jit(solution)/shard_map/reshape | solution.py:80
  4.8 0.0 copy-start.4
  4.8 0.0 copy-start.3
  4.8 0.0 copy-start.1
  4.8 7.3 %all-to-all-start = ((bf16[16,4,16,2048]{3,2,1,0:T(8,128)(2,1)}), bf16[16,4,16,2048]{3,2,1,0:T(8,128)(2,1)}, u32[]{:S(2)}, u32[]{:S(2)}) async-start(bf16[16,4,16,2048]{3,2,1,0:T(8,128)(2,1)} %bitcast.81), calls=%async_computation | async-start | bytes 8388608 | tf_op jit(solution)/shard_map/all_to_all | solution.py:81
  12.2 0.0 copy-done.4
  12.2 0.0 copy-done.3
  12.2 0.0 copy-done.1
  12.3 0.0 copy-start
  12.3 0.0 copy-start.2
  12.3 3.6 %convolution_bitcast_fusion = f32[1024,32]{0,1:T(8,128)S(1)} fusion(bf16[1024,2048]{1,0:T(8,128)(2,1)} %bitcast.82, s32[2048]{0:T(1024)S(1)} %add_select_fusion.1), kind=kOutput, calls=%fused_computation.10 | convolution fusion | flops 134348800 | bytes 4333568 | tf_op jit(solution)/shard_map/dot_general | solution.py:30
  15.9 0.1 reshape.162
  16.0 0.3 copy.26
  16.3 0.2 dot_general.33
  16.6 1.3 fusion.8
  17.9 72.2 %all-gather = f32[16,4,1200]{2,1,0:T(4,128)S(1)} all-gather(f32[1,4,1200]{2,1,0:T(4,128)S(1)} %multiply_bitcast_fusion), channel_id=1, replica_groups=mesh['mem'=16,'pix'=8] {'mem'}, dimensions={0}, use_global_device_ids=true | all-gather | bytes 326400 | tf_op jit(solution)/shard_map/all_gather | solution.py:87
  90.1 0.1 reshape.166
  90.3 0.1 reduce_sum.37
  90.3 0.0 copy-done
  90.3 0.0 copy-done.2
  90.4 0.1 fusion.24
  90.5 0.9 fusion.15
  91.4 25.5 %psum.7 = f32[64,192]{0,1:T(8,128)S(1)} all-reduce(f32[64,192]{0,1:T(8,128)S(1)} %fusion.15), channel_id=1, replica_groups=mesh['mem'=16,'pix'=8] {'pix'}, use_global_device_ids=true, to_apply=%region_2.3 | all-reduce | flops 12288 | bytes 98304 | tf_op jit(solution)/shard_map/psum | solution.py:101
  116.9 0.1 copy.28
  117.0 5.8 %cholesky.44 = f32[64,64]{1,0:T(8,128)S(1)} custom-call(f32[64,64]{1,0:T(8,128)S(1)} %fusion.43), custom_call_target="Cholesky" | custom-call | tf_op jit(solution)/shard_map/jit(cholesky)/cholesky | solution.py:50
  122.9 0.7 compare_reduce_fusion.1
  123.7 0.7 fusion.33
  124.4 4.9 %custom-call.8 = f32[1,64,64]{1,2,0:T(8,128)S(1)} custom-call(f32[1,64,64]{2,1,0:T(8,128)S(1)} %fusion.33), custom_call_target="InvertDiagBlocksLowerTriangular" | custom-call | tf_op jit(solution)/shard_map/jit(_cho_solve)/triangular_solve | solution.py:51
  129.3 0.2 fusion.35
  129.5 0.3 fusion.26
  129.8 0.2 fusion.31
  130.0 0.2 convolution_add_fusion.1
  130.3 0.1 copy.31
  130.4 5.8 %cholesky.55 = f32[64,64]{1,0:T(8,128)S(1)} custom-call(f32[64,64]{1,0:T(8,128)S(1)} %fusion.40), custom_call_target="Cholesky" | custom-call | tf_op jit(solution)/shard_map/jit(cholesky)/cholesky | solution.py:50
  136.2 0.7 compare_reduce_fusion
  137.0 0.7 fusion.34
  137.7 4.9 %custom-call.9 = f32[1,64,64]{1,2,0:T(8,128)S(1)} custom-call(f32[1,64,64]{2,1,0:T(8,128)S(1)} %fusion.34), custom_call_target="InvertDiagBlocksLowerTriangular" | custom-call | tf_op jit(solution)/shard_map/jit(_cho_solve)/triangular_solve | solution.py:51
  142.6 0.1 fusion.11
  142.7 0.2 fusion.28
  142.9 0.2 fusion.38
  143.2 0.2 fusion.13
  143.4 0.3 fusion.60
  143.7 0.1 fusion.46
  143.8 5.9 %broadcast_multiply_fusion = bf16[64,16,64,16]{3,2,1,0:T(8,128)(2,1)} fusion(bf16[16,16]{1,0:T(8,128)(2,1)S(1)} %fusion.56, bf16[64,64]{1,0:T(8,128)(2,1)S(1)} %fusion.46), kind=kLoop, calls=%fused_computation.1 | loop fusion | flops 1048576 | bytes 2105856 | tf_op jit(solution)/shard_map/mul | solution.py:107
  149.7 29.1 %mul.60 = bf16[1024,1024]{1,0:T(8,128)(2,1)S(1)} reshape(bf16[64,16,64,16]{3,2,1,0:T(8,128)(2,1)} %broadcast_multiply_fusion) | data formatting | bytes 4194304 | tf_op jit(solution)/shard_map/mul | solution.py:107
  178.8 0.0 all-to-all-done
  178.8 8.0 %add_convert_fusion = bf16[1024,2048]{1,0:T(8,128)(2,1)S(1)} fusion(bf16[1024,2048]{1,0:T(8,128)(2,1)} %bitcast.1, bf16[1024,1024]{1,0:T(8,128)(2,1)S(1)} %mul.60), kind=kOutput, calls=%fused_computation | convolution fusion | flops 4301258752 | bytes 10485760 | tf_op jit(solution)/shard_map/dot_general | solution.py:110
  186.9 53.3 %all_to_all.10 = bf16[16,4,16,2048]{3,2,1,0:T(8,128)(2,1)S(1)} all-to-all(bf16[16,4,16,2048]{3,2,1,0:T(8,128)(2,1)S(1)} %bitcast.85), channel_id=1, replica_groups=mesh['mem'=16,'pix'=8] {'mem'}, dimensions={0} | all-to-all | bytes 8388608 | tf_op jit(solution)/shard_map/all_to_all | solution.py:113
  240.2 2.3 copy.43
  (16 shorter events, 0.2 us)
Async XLA Ops:
  4.8 7.4 %copy-start.4 = (s32[1200]{0:T(1024)S(1)}, s32[1200]{0:T(1024)}, u32[]{:S(2)}) copy-start(s32[1200]{0:T(1024)} %param.14) | copy-start | bytes 14404
  4.8 7.4 %copy-start.3 = (f32[1200]{0:T(1024)S(1)}, f32[1200]{0:T(1024)}, u32[]{:S(2)}) copy-start(f32[1200]{0:T(1024)} %param.11) | copy-start | bytes 14404
  4.8 7.4 %copy-start.1 = (s32[2,1200]{1,0:T(2,128)S(1)}, s32[2,1200]{1,0:T(2,128)}, u32[]{:S(2)}) copy-start(s32[2,1200]{1,0:T(2,128)} %param.13) | copy-start | bytes 28804
  4.8 174.0 %all-to-all-start = ((bf16[16,4,16,2048]{3,2,1,0:T(8,128)(2,1)}), bf16[16,4,16,2048]{3,2,1,0:T(8,128)(2,1)}, u32[]{:S(2)}, u32[]{:S(2)}) async-start(bf16[16,4,16,2048]{3,2,1,0:T(8,128)(2,1)} %bitcast.81), calls=%async_computation | async-start | bytes 8388608 | tf_op jit(solution)/shard_map/all_to_all | solution.py:81
  12.3 78.1 %copy-start = (f32[2,1200,64]{1,2,0:T(8,128)S(1)}, f32[2,1200,64]{1,2,0:T(8,128)}, u32[]{:S(2)}) copy-start(f32[2,1200,64]{1,2,0:T(8,128)} %param.12) | copy-start | bytes 1843204
  12.3 78.1 %copy-start.2 = (f32[1200]{0:T(1024)S(1)}, f32[1200]{0:T(1024)}, u32[]{:S(2)}) copy-start(f32[1200]{0:T(1024)} %param.10) | copy-start | bytes 14404
